TPU v7x, 256 devices: a whole 4x4x8 slice. The times are simulated.
256 devices in a mesh: row: 8 (over x, core), col: 32 (over y, z).
Axes of the slice: x: 4, y: 4, z: 8, core: 2. Of those that a mesh axis runs over, the one named last changes fastest.
Arguments:
- tensor: float32 [1024, 64, 4096], P(None, 'row', 'col'), may hold values from -60 to 60, as said below
- factor_two: float32 [64, 32], P('row'), may hold values from -0.75 to 0.75
- factor_three: float32 [128, 32], P('col'), may hold values from -0.5 to 0.5
- factor_four: float32 [32, 16], replicated, may hold values from -1 to 1
- factor_init: float32 [1024, 64], replicated, may hold values from -6 to 6
Outputs:
- factor_new: float32 [1024, 64], replicated
- core: float32 [64, 32, 32, 16], P(None, 'row', 'col')
Inputs may be any that keep to these rules, and one draw needn't show every extreme that they name: `tensor`: scales vary from slab to slab.
All inputs are finite; a program needn't handle non-finite values.
Results may differ from a plain program's by a relative error of at most 0.00013.
Values sent between devices are 32-bit elements; how exact they have to be, the bound alone decides.
No kernel may reach another device: no remote copies, remote signals or barrier semaphores. Data moves between devices by JAX's collectives and lax.ppermute only.
A program may use at most 128 MiB of HBM per device.

v0:
```python
import jax
import jax.numpy as jnp
from jax import lax
from jax.sharding import Mesh
from jax.sharding import PartitionSpec as P

ROW = ("row_0", "row_1")
COL = ("col_0", "col_1")


def from_everyone(array, axis):
    copies = jnp.broadcast_to(array, (lax.axis_size(axis), *array.shape))
    return lax.all_to_all(copies, axis, split_axis=0, concat_axis=0, tiled=True)


def joined_along(tiles, dim):
    shape = list(tiles.shape[1:])
    shape[dim] *= tiles.shape[0]
    return jnp.moveaxis(tiles, 0, dim).reshape(shape)


def gathered_copies(array, axis, dim):
    tiles = from_everyone(array, axis)
    return joined_along(tiles, dim)


def split_up(array, dim, length):
    shape = array.shape
    tiles = array.reshape(*shape[:dim], length, shape[dim] // length, *shape[dim + 1 :])
    return jnp.moveaxis(tiles, dim, 0)


def sent_and_summed(array, axis, dim):
    tiles = split_up(array, dim, lax.axis_size(axis))
    arrived = lax.all_to_all(tiles, axis, split_axis=0, concat_axis=0, tiled=True)
    return arrived.sum(axis=0)


def sum_by_axis(array, axes, dim):
    far, near = axes
    tiles = split_up(array, dim, lax.axis_size(far))
    nearer = sent_and_summed(tiles, near, dim + 1)
    arrived = lax.all_to_all(nearer, far, split_axis=0, concat_axis=0, tiled=True)
    return arrived.sum(axis=0)


def rows_for(lines, length):
    spare = -lines.shape[0] % length
    if not spare:
        return lines
    return jnp.concatenate([lines, jnp.zeros((spare, *lines.shape[1:]), lines.dtype)])


def gathered_by_axis(array, axes, dim):
    far, near = axes
    leading = from_everyone(array, far)
    tiles = jnp.swapaxes(from_everyone(leading, near), 0, 1)
    return joined_along(tiles.reshape(-1, *array.shape), dim)


def nested_sum(array, axes):
    lines = array.reshape(-1, array.shape[-1])
    own = sum_by_axis(rows_for(lines, lax.axis_size(axes[0]) * lax.axis_size(axes[1])), axes, 0)
    whole = gathered_by_axis(own, axes, 0)
    return whole[: len(lines)].reshape(array.shape)


def shards(tensor, factor_two, factor_three, factor_four, factor_init):
    highest = lax.Precision.HIGHEST
    first_len = tensor.shape[0]
    local_two = tensor.shape[1]
    fourth_len = factor_four.shape[0]
    local_three = tensor.shape[2] // fourth_len
    rank_one = factor_init.shape[1]
    data = tensor.reshape(first_len, local_two, local_three, fourth_len)
    fourth = jnp.einsum("abcd,de->abce", data, factor_four, precision=highest)
    whole_two = gathered_copies(factor_two, ROW, 0)
    spread_two = lax.all_to_all(fourth, ROW, split_axis=0, concat_axis=1, tiled=True)
    projected_two = jnp.einsum("abce,bg->agce", spread_two, whole_two, precision=highest)
    partial_two = lax.all_to_all(projected_two, ROW, split_axis=1, concat_axis=0, tiled=True)
    whole_three = gathered_copies(factor_three, COL, 0)
    spread_three = lax.all_to_all(partial_two, COL, split_axis=0, concat_axis=2, tiled=True)
    projected_three = jnp.einsum("agce,cf->agfe", spread_three, whole_three, precision=highest)
    block = lax.all_to_all(projected_three, COL, split_axis=2, concat_axis=0, tiled=True)
    columns = block.reshape(first_len, -1)
    basis = factor_init
    inner = jnp.dot(columns.T, basis, precision=highest, preferred_element_type=jnp.float32)
    local_image = jnp.dot(columns, inner, precision=highest, preferred_element_type=jnp.float32)
    image = nested_sum(local_image, (("row_0", "row_1"), ("col_0", "col_1")))
    square = jnp.dot(image.T, image, precision=highest, preferred_element_type=jnp.float32)
    lower = jnp.linalg.cholesky(square)
    basis = jax.scipy.linalg.solve_triangular(lower, image.T, lower=True).T
    core = jnp.dot(basis.T, columns, precision=highest, preferred_element_type=jnp.float32)
    return (basis, core.reshape(rank_one, block.shape[1], block.shape[2], block.shape[3]))


def solution(mesh):
    split = Mesh(mesh.devices.reshape(4, 2, 4, 8), ("row_0", "row_1", "col_0", "col_1"))
    in_specs = (P(None, ROW, COL), P(ROW, None), P(COL, None), P(), P())
    out_specs = (P(), P(None, ROW, COL, None))
    return jax.shard_map(
        shards, mesh=split, in_specs=in_specs, out_specs=out_specs, check_vma=False
    )
```

profile of v0, /device:TPU:32, one launch (start us, length us, event | category | flops | bytes accessed | tf_op | source)
XLA Modules:
  0.0 319.9 jit_solution(13342368360743462871)
XLA Ops:
  0.6 0.7 broadcast_in_dim.14
  1.4 0.7 reshape.45
  2.1 4.3 %all-to-all-start.1 = ((f32[8,1,256]{2,1,0:T(1,128)}), f32[8,1,256]{2,1,0:T(1,128)S(1)}, u32[]{:S(2)}, u32[]{:S(2)}) async-start(f32[8,1,256]{2,1,0:T(1,128)} %reshape.45), calls=%async_computation.1 | async-start | bytes 16384 | tf_op jit(solution)/shard_map/all_to_all | solution.py:13
  6.4 5.4 %copy.77 = f32[1024,8,128]{0,2,1:T(8,128)} copy(f32[1024,8,128]{2,1,0:T(8,128)} %param.5) | data formatting | bytes 8388608 | tf_op args[0]
  11.8 4.2 %fusion.18 = f32[1024,8,4,16]{0,3,2,1:T(8,128)S(1)} fusion(f32[1024,8,4,32]{0,3,2,1:T(8,128)} %bitcast.92, f32[32,16]{0,1:T(8,128)S(1)} %copy-done.2), kind=kOutput, calls=%fused_computation.24 | convolution fusion | flops 201326592 | bytes 6293504 | tf_op jit(solution)/shard_map/abcd,de->abce/dot_general | solution.py:76
  16.0 12.2 %copy.78 = f32[1024,8,4,16]{3,2,1,0:T(4,128)} copy(f32[1024,8,4,16]{0,3,2,1:T(8,128)S(1)} %fusion.18) | data formatting | bytes 4194304 | tf_op jit(solution)/shard_map/abcd,de->abce/dot_general | solution.py:76
  28.1 15.4 %reshape.43 = f32[8,1,65536]{2,1,0:T(1,128)} reshape(f32[1024,8,4,16]{3,2,1,0:T(4,128)} %copy.78) | data formatting | bytes 4194304
  43.5 5.3 %all-to-all-start = ((f32[8,1,65536]{2,1,0:T(1,128)}), f32[8,1,65536]{2,1,0:T(1,128)}, u32[]{:S(2)}, u32[]{:S(2)}) async-start(f32[8,1,65536]{2,1,0:T(1,128)} %reshape.43), calls=%async_computation | async-start | bytes 4194304 | tf_op jit(solution)/shard_map/all_to_all | solution.py:78
  49.3 0.7 reduce.7
  50.1 25.5 %all-to-all-done = f32[8,1,65536]{2,1,0:T(1,128)} async-done(((f32[8,1,65536]{2,1,0:T(1,128)}), f32[8,1,65536]{2,1,0:T(1,128)}, u32[]{:S(2)}, u32[]{:S(2)}) %all-to-all-start) | async-done | bytes 2097184 | tf_op jit(solution)/shard_map/all_to_all | solution.py:78
  75.6 7.2 %reduce.6 = f32[8,65536]{1,0:T(8,128)S(1)} reduce(f32[8,1,65536]{2,1,0:T(1,128)} %all-to-all-done, f32[]{:T(128)} %broadcast.53), dimensions={1}, to_apply=%all_to_all.64.reduce_sub_computation | reduce | bytes 4194308 | tf_op jit(solution)/shard_map/all_to_all | solution.py:78
  82.8 17.3 %reshape.44 = f32[1024,8,4,16]{3,2,1,0:T(4,128)} reshape(f32[8,65536]{1,0:T(8,128)S(1)} %reduce.6) | data formatting | bytes 4194304
  100.1 10.0 %copy.106 = f32[8,128,8,4,16]{1,0,3,4,2:T(8,128)S(1)} copy(f32[8,128,8,4,16]{4,3,2,1,0:T(4,128)} %bitcast.89) | data formatting | bytes 4194304 | tf_op jit(solution)/shard_map/all_to_all | solution.py:78
  110.1 1.4 fusion.4
  111.5 1.6 copy.81
  113.1 3.6 %all-to-all-start.2 = ((f32[128,32,4,16]{0,3,2,1:T(8,128)}), f32[128,32,4,16]{0,3,2,1:T(8,128)S(1)}, u32[]{:S(2)}, u32[]{:S(2)}) async-start(f32[128,32,4,16]{0,3,2,1:T(8,128)} %copy.81), calls=%async_computation.2 | async-start | bytes 2097152 | tf_op jit(solution)/shard_map/all_to_all | solution.py:80
  116.7 0.7 reshape.49
  117.4 15.1 %all-to-all-done.2 = f32[128,32,4,16]{0,3,2,1:T(8,128)S(1)} async-done(((f32[128,32,4,16]{0,3,2,1:T(8,128)}), f32[128,32,4,16]{0,3,2,1:T(8,128)S(1)}, u32[]{:S(2)}, u32[]{:S(2)}) %all-to-all-start.2) | async-done | bytes 1048608 | tf_op jit(solution)/shard_map/all_to_all | solution.py:80
  132.5 11.4 %all-to-all-start.4 = ((f32[32,1,128]{2,1,0:T(1,128)}), f32[32,1,128]{2,1,0:T(1,128)S(1)}, u32[]{:S(2)}, u32[]{:S(2)}) async-start(f32[32,1,128]{2,1,0:T(1,128)} %reshape.49), calls=%async_computation.4 | async-start | bytes 32768 | tf_op jit(solution)/shard_map/all_to_all | solution.py:13
  143.8 6.1 %copy.110 = f32[8,128,4,4,16]{4,3,2,1,0:T(4,128)} copy(f32[8,128,4,4,16]{1,4,3,2,0:T(8,128)S(1)} %bitcast.93) | data formatting | bytes 2097152 | tf_op jit(solution)/shard_map/all_to_all | solution.py:80
  150.0 8.9 %reshape.47 = f32[32,1,8192]{2,1,0:T(1,128)} reshape(f32[1024,4,4,16]{3,2,1,0:T(4,128)} %bitcast.90) | data formatting | bytes 2097152
  158.9 10.1 %all-to-all-start.3 = ((f32[32,1,8192]{2,1,0:T(1,128)}), f32[32,1,8192]{2,1,0:T(1,128)S(1)}, u32[]{:S(2)}, u32[]{:S(2)}) async-start(f32[32,1,8192]{2,1,0:T(1,128)} %reshape.47), calls=%async_computation.3 | async-start | bytes 2097152 | tf_op jit(solution)/shard_map/all_to_all | solution.py:82
  169.0 0.7 reduce.9
  169.8 26.8 %all-to-all-done.3 = f32[32,1,8192]{2,1,0:T(1,128)S(1)} async-done(((f32[32,1,8192]{2,1,0:T(1,128)}), f32[32,1,8192]{2,1,0:T(1,128)S(1)}, u32[]{:S(2)}, u32[]{:S(2)}) %all-to-all-start.3) | async-done | bytes 1048608 | tf_op jit(solution)/shard_map/all_to_all | solution.py:82
  196.6 3.2 %reduce.8 = f32[32,8192]{1,0:T(8,128)S(1)} reduce(f32[32,1,8192]{2,1,0:T(1,128)S(1)} %all-to-all-done.3, f32[]{:T(128)} %broadcast.53), dimensions={1}, to_apply=%all_to_all.72.reduce_sub_computation | reduce | bytes 2097156 | tf_op jit(solution)/shard_map/all_to_all | solution.py:82
  199.8 7.2 %reshape.48 = f32[1024,4,4,16]{3,2,1,0:T(4,128)} reshape(f32[32,8192]{1,0:T(8,128)S(1)} %reduce.8) | data formatting | bytes 2097152
  207.1 10.0 %copy.85 = f32[32,32,4,4,16]{0,1,3,4,2:T(8,128)} copy(f32[32,32,4,4,16]{4,3,2,1,0:T(4,128)} %bitcast.91) | data formatting | bytes 2097152 | tf_op jit(solution)/shard_map/all_to_all | solution.py:82
  217.1 5.6 %fusion.7 = f32[32,4,32,16]{2,0,3,1:T(8,128)S(1)} fusion(f32[32,32,4,4,16]{0,1,3,4,2:T(8,128)} %copy.85, f32[32,4,32,1,1]{2,1,0,4,3:T(4,128)S(1)} %bitcast.99), kind=kOutput, calls=%fused_computation.5 | convolution fusion | flops 100663296 | bytes 1327104 | tf_op jit(solution)/shard_map/agce,cf->agfe/dot_general | solution.py:83
  222.7 0.9 copy.87
  224.1 16.8 %all_to_all.93 = f32[32,1,2048]{2,1,0:T(1,128)S(1)} all-to-all(f32[32,1,2048]{2,1,0:T(1,128)S(1)} %reshape.51), channel_id=1, replica_groups=mesh['row_0'=4,'row_1'=2,'col_0'=4,'col_1'=8] {'col_0','col_1'}, dimensions={0} | all-to-all | bytes 524288 | tf_op jit(solution)/shard_map/all_to_all | solution.py:84
  240.9 1.3 reduce.10
  242.6 1.6 copy.89
  244.2 0.9 copy.88
  245.1 1.7 reshape.33
  246.9 1.0 dot_general.30
  249.7 15.8 %all_to_all.94 = f32[32,1,2048]{2,1,0:T(1,128)S(1)} all-to-all(f32[32,1,2048]{2,1,0:T(1,128)S(1)} %reshape.53), channel_id=1, replica_groups=mesh['row_0'=4,'row_1'=2,'col_0'=4,'col_1'=8] {'col_0','col_1'}, dimensions={0} | all-to-all | bytes 524288 | tf_op jit(solution)/shard_map/all_to_all | solution.py:35
  265.5 1.3 reduce.11
  267.3 7.7 %all_to_all.95 = f32[8,1,256]{2,1,0:T(1,128)S(1)} all-to-all(f32[8,1,256]{2,1,0:T(1,128)S(1)} %reshape.55), channel_id=1, replica_groups=mesh['row_0'=4,'row_1'=2,'col_0'=4,'col_1'=8] {'row_0','row_1'}, dimensions={0} | all-to-all | bytes 16384 | tf_op jit(solution)/shard_map/all_to_all | solution.py:43
  275.0 0.7 reduce.12
  275.9 7.7 %all_to_all.96 = f32[8,1,256]{2,1,0:T(1,128)S(1)} all-to-all(f32[8,1,256]{2,1,0:T(1,128)S(1)} %reshape.57), channel_id=1, replica_groups=mesh['row_0'=4,'row_1'=2,'col_0'=4,'col_1'=8] {'row_0','row_1'}, dimensions={0} | all-to-all | bytes 16384 | tf_op jit(solution)/shard_map/all_to_all | solution.py:13
  283.5 0.7 reduce.13
  284.9 16.9 %all_to_all.97 = f32[32,1,2048]{2,1,0:T(1,128)S(1)} all-to-all(f32[32,1,2048]{2,1,0:T(1,128)S(1)} %reshape.59), channel_id=1, replica_groups=mesh['row_0'=4,'row_1'=2,'col_0'=4,'col_1'=8] {'col_0','col_1'}, dimensions={0} | all-to-all | bytes 524288 | tf_op jit(solution)/shard_map/all_to_all | solution.py:13
  301.8 1.3 reduce.14
  303.4 1.4 convolution_bitcast_fusion.1
  305.2 5.8 %cholesky.16 = f32[64,64]{1,0:T(8,128)S(1)} custom-call(f32[64,64]{1,0:T(8,128)S(1)} %fusion.16), custom_call_target="Cholesky" | custom-call | tf_op jit(solution)/shard_map/jit(cholesky)/cholesky | solution.py:91
  312.4 4.9 %custom-call.7 = f32[1,64,64]{1,2,0:T(8,128)S(1)} custom-call(f32[1,64,64]{2,1,0:T(8,128)S(1)} %fusion.13), custom_call_target="InvertDiagBlocksLowerTriangular" | custom-call | tf_op jit(solution)/shard_map/jit(_solve_triangular)/triangular_solve | solution.py:92
  317.7 0.7 fusion.14
  318.4 1.0 convolution_bitcast_fusion.2
  (39 shorter events, 7.2 us)
Async XLA Ops:
  0.6 247.3 %copy-start = (f32[1024,64]{0,1:T(8,128)S(1)}, f32[1024,64]{0,1:T(8,128)}, u32[]{:S(2)}) copy-start(f32[1024,64]{0,1:T(8,128)} %param.9) | copy-start | bytes 786436
  2.1 41.5 %all-to-all-start.1 = ((f32[8,1,256]{2,1,0:T(1,128)}), f32[8,1,256]{2,1,0:T(1,128)S(1)}, u32[]{:S(2)}, u32[]{:S(2)}) async-start(f32[8,1,256]{2,1,0:T(1,128)} %reshape.45), calls=%async_computation.1 | async-start | bytes 16384 | tf_op jit(solution)/shard_map/all_to_all | solution.py:13
  6.4 5.4 %copy-start.2 = (f32[32,16]{0,1:T(8,128)S(1)}, f32[32,16]{0,1:T(8,128)}, u32[]{:S(2)}) copy-start(f32[32,16]{0,1:T(8,128)} %param.8) | copy-start | bytes 6148
  43.5 32.1 %all-to-all-start = ((f32[8,1,65536]{2,1,0:T(1,128)}), f32[8,1,65536]{2,1,0:T(1,128)}, u32[]{:S(2)}, u32[]{:S(2)}) async-start(f32[8,1,65536]{2,1,0:T(1,128)} %reshape.43), calls=%async_computation | async-start | bytes 4194304 | tf_op jit(solution)/shard_map/all_to_all | solution.py:78
  110.1 6.5 %copy-start.3 = (f32[4,32]{1,0:T(4,128)S(1)}, f32[4,32]{1,0:T(4,128)}, u32[]{:S(2)}) copy-start(f32[4,32]{1,0:T(4,128)} %param.7) | copy-start | bytes 1540
  113.1 19.4 %all-to-all-start.2 = ((f32[128,32,4,16]{0,3,2,1:T(8,128)}), f32[128,32,4,16]{0,3,2,1:T(8,128)S(1)}, u32[]{:S(2)}, u32[]{:S(2)}) async-start(f32[128,32,4,16]{0,3,2,1:T(8,128)} %copy.81), calls=%async_computation.2 | async-start | bytes 2097152 | tf_op jit(solution)/shard_map/all_to_all | solution.py:80
  132.5 26.4 %all-to-all-start.4 = ((f32[32,1,128]{2,1,0:T(1,128)}), f32[32,1,128]{2,1,0:T(1,128)S(1)}, u32[]{:S(2)}, u32[]{:S(2)}) async-start(f32[32,1,128]{2,1,0:T(1,128)} %reshape.49), calls=%async_computation.4 | async-start | bytes 32768 | tf_op jit(solution)/shard_map/all_to_all | solution.py:13
  158.9 37.7 %all-to-all-start.3 = ((f32[32,1,8192]{2,1,0:T(1,128)}), f32[32,1,8192]{2,1,0:T(1,128)S(1)}, u32[]{:S(2)}, u32[]{:S(2)}) async-start(f32[32,1,8192]{2,1,0:T(1,128)} %reshape.47), calls=%async_computation.3 | async-start | bytes 2097152 | tf_op jit(solution)/shard_map/all_to_all | solution.py:82
  318.4 1.0 copy-start.1
where the time goes:
time: 325 us; the launch traced here: 320 us
  local copies, waits for them, and re-layouts  107 us (33%)
  waiting for transfers between devices  67.4 us (21%)
  blocking collectives  64.8 us (20%)
  starting transfers between devices  34.6 us (11%)
  other arithmetic  29.1 us (9%)
  matrix products  15.2 us (5%)
    unnamed x27, local copies, waits for them, and re-layouts  58.6 us
    all_to_all x1, waiting for transfers between devices, shards(): lax.all_to_all(partial_two, COL, split_axis=0, concat_axis=2, tiled=True)  26.8 us
    all_to_all x1, waiting for transfers between devices, shards(): lax.all_to_all(fourth, ROW, split_axis=0, concat_axis=1, tiled=True)  25.5 us
    all_to_all x2, blocking collectives, from_everyone(): return lax.all_to_all(copies, axis, split_axis=0, concat_axis=0, tiled=True)  24.5 us
    all_to_all x1, blocking collectives, shards(): lax.all_to_all(projected_three, COL, split_axis=2, concat_axis=0, tiled=T...  16.8 us
    all_to_all x1, blocking collectives, sent_and_summed(): lax.all_to_all(tiles, axis, split_axis=0, concat_axis=0, tiled=True)  15.8 us
    all_to_all x2, starting transfers between devices, from_everyone(): return lax.all_to_all(copies, axis, split_axis=0, concat_axis=0, tiled=True)  15.7 us
    all_to_all x1, waiting for transfers between devices, shards(): lax.all_to_all(projected_two, ROW, split_axis=1, concat_axis=0, tiled=True)  15.1 us
  transfers between devices with their start and end apart: 5, of which 3 were waited for; matrix products, arithmetic and copies ran while one was open for 17% of the time, Pallas kernels for 0%

commit v1 on v0

--- a/solution.py
+++ b/solution.py
@@ -75,7 +75,9 @@
     data = tensor.reshape(first_len, local_two, local_three, fourth_len)
     fourth = jnp.einsum("abcd,de->abce", data, factor_four, precision=highest)
     whole_two = gathered_copies(factor_two, ROW, 0)
-    spread_two = lax.all_to_all(fourth, ROW, split_axis=0, concat_axis=1, tiled=True)
+    spread_two = jnp.concatenate(
+        lax.all_to_all(jnp.stack(jnp.split(fourth, lax.axis_size(ROW), axis=0)), ROW, 0, 0), axis=1
+    )
     projected_two = jnp.einsum("abce,bg->agce", spread_two, whole_two, precision=highest)
     partial_two = lax.all_to_all(projected_two, ROW, split_axis=1, concat_axis=0, tiled=True)
     whole_three = gathered_copies(factor_three, COL, 0)

time: 325 us -> 260 us (0.80); the launches traced: 320 us -> 259 us
  local copies, waits for them, and re-layouts: 107 us -> 54.1 us
  other arithmetic: 29.1 us -> 21.9 us
    unnamed x27 -> x34, local copies, waits for them, and re-layouts: 58.6 us -> 27.5 us
    dot_general x1 -> x0, local copies, waits for them, and re-layouts: 12.2 us -> none  [shards(): fourth = jnp.einsum('abcd,de->abce', data, factor_four, precision=highest)]
    all_to_all x2 -> x0, local copies, waits for them, and re-layouts: 10.5 us -> none  [shards(): lax.all_to_all(fourth, ROW, split_axis=0, concat_axis=1, tiled=True)]
    all_to_all x1 -> x0, other arithmetic: 7.22 us -> none  [shards(): lax.all_to_all(fourth, ROW, split_axis=0, concat_axis=1, tiled=True)]
  transfers between devices with their start and end apart: 5 -> 5, of which waited for: 3 -> 3; matrix products, arithmetic and copies ran while one was open for 17% -> 11% of each run, Pallas kernels for 0% -> 0%
where the time goes in v1:
time: 260 us; the launch traced here: 259 us
  waiting for transfers between devices  68 us (26%)
  blocking collectives  64.3 us (25%)
  local copies, waits for them, and re-layouts  54.1 us (21%)
  starting transfers between devices  33.8 us (13%)
  other arithmetic  21.9 us (8%)
  matrix products  16.3 us (6%)
    unnamed x34, local copies, waits for them, and re-layouts  27.5 us
    all_to_all x1, waiting for transfers between devices, shards(): lax.all_to_all(partial_two, COL, split_axis=0, concat_axis=2, tiled=True)  26.9 us
    all_to_all x1, waiting for transfers between devices, shards(): lax.all_to_all(jnp.stack(jnp.split(fourth, lax.axis_size(ROW), axis=0)),...  25.9 us
    all_to_all x2, blocking collectives, from_everyone(): return lax.all_to_all(copies, axis, split_axis=0, concat_axis=0, tiled=True)  24.3 us
    all_to_all x1, blocking collectives, shards(): lax.all_to_all(projected_three, COL, split_axis=2, concat_axis=0, tiled=T...  16.5 us
    all_to_all x1, blocking collectives, sent_and_summed(): lax.all_to_all(tiles, axis, split_axis=0, concat_axis=0, tiled=True)  15.8 us
    all_to_all x2, starting transfers between devices, from_everyone(): return lax.all_to_all(copies, axis, split_axis=0, concat_axis=0, tiled=True)  15.7 us
    all_to_all x1, waiting for transfers between devices, shards(): lax.all_to_all(projected_two, ROW, split_axis=1, concat_axis=0, tiled=True)  15.1 us
  transfers between devices with their start and end apart: 5, of which 3 were waited for; matrix products, arithmetic and copies ran while one was open for 11% of the time, Pallas kernels for 0%

profile of v1, /device:TPU:32, one launch (start us, length us, event | category | flops | bytes accessed | tf_op | source)
XLA Modules:
  0.0 259.4 jit_solution(12607006318543335760)
XLA Ops:
  0.6 0.7 broadcast_in_dim.14
  1.4 0.7 reshape.48
  2.1 4.3 %all-to-all-start.1 = ((f32[8,1,256]{2,1,0:T(1,128)}), f32[8,1,256]{2,1,0:T(1,128)S(1)}, u32[]{:S(2)}, u32[]{:S(2)}) async-start(f32[8,1,256]{2,1,0:T(1,128)} %reshape.48), calls=%async_computation.1 | async-start | bytes 16384 | tf_op jit(solution)/shard_map/all_to_all | solution.py:13
  6.4 5.4 %copy.55 = f32[1024,8,128]{0,2,1:T(8,128)} copy(f32[1024,8,128]{2,1,0:T(8,128)} %param.5) | data formatting | bytes 8388608 | tf_op args[0]
  11.8 4.2 %fusion.26 = f32[1024,8,4,16]{0,3,2,1:T(8,128)S(1)} fusion(f32[1024,8,4,32]{0,3,2,1:T(8,128)} %bitcast.122, f32[32,16]{0,1:T(8,128)S(1)} %copy-done.3), kind=kOutput, calls=%fused_computation.40 | convolution fusion | flops 201326592 | bytes 6293504 | tf_op jit(solution)/shard_map/abcd,de->abce/dot_general | solution.py:76
  16.3 1.3 copy-done.1
  17.7 4.8 %all-to-all-start = ((f32[8,128,8,4,16]{1,4,3,2,0:T(8,128)}), f32[8,128,8,4,16]{1,4,3,2,0:T(8,128)S(1)}, u32[]{:S(2)}, u32[]{:S(2)}) async-start(f32[8,128,8,4,16]{1,4,3,2,0:T(8,128)} %copy-done.1), calls=%async_computation | async-start | bytes 4194304 | tf_op jit(solution)/shard_map/all_to_all | solution.py:79
  22.5 0.5 broadcast.53
  23.0 0.7 reduce.6
  23.7 25.9 %all-to-all-done = f32[8,128,8,4,16]{1,4,3,2,0:T(8,128)S(1)} async-done(((f32[8,128,8,4,16]{1,4,3,2,0:T(8,128)}), f32[8,128,8,4,16]{1,4,3,2,0:T(8,128)S(1)}, u32[]{:S(2)}, u32[]{:S(2)}) %all-to-all-start) | async-done | bytes 2097184 | tf_op jit(solution)/shard_map/all_to_all | solution.py:79
  49.6 2.5 fusion.4
  52.1 1.6 copy.57
  53.7 3.6 %all-to-all-start.2 = ((f32[128,32,4,16]{0,3,2,1:T(8,128)}), f32[128,32,4,16]{0,3,2,1:T(8,128)S(1)}, u32[]{:S(2)}, u32[]{:S(2)}) async-start(f32[128,32,4,16]{0,3,2,1:T(8,128)} %copy.57), calls=%async_computation.2 | async-start | bytes 2097152 | tf_op jit(solution)/shard_map/all_to_all | solution.py:82
  57.3 0.7 reshape.52
  58.0 15.1 %all-to-all-done.2 = f32[128,32,4,16]{0,3,2,1:T(8,128)S(1)} async-done(((f32[128,32,4,16]{0,3,2,1:T(8,128)}), f32[128,32,4,16]{0,3,2,1:T(8,128)S(1)}, u32[]{:S(2)}, u32[]{:S(2)}) %all-to-all-start.2) | async-done | bytes 1048608 | tf_op jit(solution)/shard_map/all_to_all | solution.py:82
  73.2 11.4 %all-to-all-start.4 = ((f32[32,1,128]{2,1,0:T(1,128)}), f32[32,1,128]{2,1,0:T(1,128)S(1)}, u32[]{:S(2)}, u32[]{:S(2)}) async-start(f32[32,1,128]{2,1,0:T(1,128)} %reshape.52), calls=%async_computation.4 | async-start | bytes 32768 | tf_op jit(solution)/shard_map/all_to_all | solution.py:13
  84.5 6.1 %copy.80 = f32[8,128,4,4,16]{4,3,2,1,0:T(4,128)} copy(f32[8,128,4,4,16]{1,4,3,2,0:T(8,128)S(1)} %bitcast.124) | data formatting | bytes 2097152 | tf_op jit(solution)/shard_map/all_to_all | solution.py:82
  90.6 8.9 %reshape.50 = f32[32,1,8192]{2,1,0:T(1,128)} reshape(f32[1024,4,4,16]{3,2,1,0:T(4,128)} %bitcast.120) | data formatting | bytes 2097152
  99.6 9.8 %all-to-all-start.3 = ((f32[32,1,8192]{2,1,0:T(1,128)}), f32[32,1,8192]{2,1,0:T(1,128)S(1)}, u32[]{:S(2)}, u32[]{:S(2)}) async-start(f32[32,1,8192]{2,1,0:T(1,128)} %reshape.50), calls=%async_computation.3 | async-start | bytes 2097152 | tf_op jit(solution)/shard_map/all_to_all | solution.py:84
  109.4 0.7 reduce.8
  110.2 26.9 %all-to-all-done.3 = f32[32,1,8192]{2,1,0:T(1,128)S(1)} async-done(((f32[32,1,8192]{2,1,0:T(1,128)}), f32[32,1,8192]{2,1,0:T(1,128)S(1)}, u32[]{:S(2)}, u32[]{:S(2)}) %all-to-all-start.3) | async-done | bytes 1048608 | tf_op jit(solution)/shard_map/all_to_all | solution.py:84
  137.1 3.2 %reduce.7 = f32[32,8192]{1,0:T(8,128)S(1)} reduce(f32[32,1,8192]{2,1,0:T(1,128)S(1)} %all-to-all-done.3, f32[]{:T(128)} %broadcast.53), dimensions={1}, to_apply=%all_to_all.62.reduce_sub_computation | reduce | bytes 2097156 | tf_op jit(solution)/shard_map/all_to_all | solution.py:84
  140.3 7.2 %reshape.51 = f32[1024,4,4,16]{3,2,1,0:T(4,128)} reshape(f32[32,8192]{1,0:T(8,128)S(1)} %reduce.7) | data formatting | bytes 2097152
  147.6 10.0 %copy.61 = f32[32,32,4,4,16]{0,1,3,4,2:T(8,128)} copy(f32[32,32,4,4,16]{4,3,2,1,0:T(4,128)} %bitcast.121) | data formatting | bytes 2097152 | tf_op jit(solution)/shard_map/all_to_all | solution.py:84
  157.6 5.6 %fusion.7 = f32[32,4,32,16]{2,0,3,1:T(8,128)S(1)} fusion(f32[32,32,4,4,16]{0,1,3,4,2:T(8,128)} %copy.61, f32[32,4,32,1,1]{2,1,0,4,3:T(4,128)S(1)} %bitcast.130), kind=kOutput, calls=%fused_computation.5 | convolution fusion | flops 100663296 | bytes 1327104 | tf_op jit(solution)/shard_map/agce,cf->agfe/dot_general | solution.py:85
  163.2 0.9 copy.63
  164.6 16.5 %all_to_all.83 = f32[32,1,2048]{2,1,0:T(1,128)S(1)} all-to-all(f32[32,1,2048]{2,1,0:T(1,128)S(1)} %reshape.54), channel_id=1, replica_groups=mesh['row_0'=4,'row_1'=2,'col_0'=4,'col_1'=8] {'col_0','col_1'}, dimensions={0} | all-to-all | bytes 524288 | tf_op jit(solution)/shard_map/all_to_all | solution.py:86
  181.1 1.3 reduce.9
  182.8 1.6 copy.65
  184.4 0.9 copy.64
  185.4 1.7 reshape.38
  187.1 1.0 dot_general.30
  188.5 0.6 convolution_bitcast_fusion
  189.9 15.8 %all_to_all.84 = f32[32,1,2048]{2,1,0:T(1,128)S(1)} all-to-all(f32[32,1,2048]{2,1,0:T(1,128)S(1)} %reshape.56), channel_id=1, replica_groups=mesh['row_0'=4,'row_1'=2,'col_0'=4,'col_1'=8] {'col_0','col_1'}, dimensions={0} | all-to-all | bytes 524288 | tf_op jit(solution)/shard_map/all_to_all | solution.py:35
  205.7 1.3 reduce.10
  207.6 7.7 %all_to_all.85 = f32[8,1,256]{2,1,0:T(1,128)S(1)} all-to-all(f32[8,1,256]{2,1,0:T(1,128)S(1)} %reshape.58), channel_id=1, replica_groups=mesh['row_0'=4,'row_1'=2,'col_0'=4,'col_1'=8] {'row_0','row_1'}, dimensions={0} | all-to-all | bytes 16384 | tf_op jit(solution)/shard_map/all_to_all | solution.py:43
  215.2 0.7 reduce.11
  216.1 7.7 %all_to_all.86 = f32[8,1,256]{2,1,0:T(1,128)S(1)} all-to-all(f32[8,1,256]{2,1,0:T(1,128)S(1)} %reshape.60), channel_id=1, replica_groups=mesh['row_0'=4,'row_1'=2,'col_0'=4,'col_1'=8] {'row_0','row_1'}, dimensions={0} | all-to-all | bytes 16384 | tf_op jit(solution)/shard_map/all_to_all | solution.py:13
  223.8 0.7 reduce.12
  225.1 16.6 %all_to_all.87 = f32[32,1,2048]{2,1,0:T(1,128)S(1)} all-to-all(f32[32,1,2048]{2,1,0:T(1,128)S(1)} %reshape.62), channel_id=1, replica_groups=mesh['row_0'=4,'row_1'=2,'col_0'=4,'col_1'=8] {'col_0','col_1'}, dimensions={0} | all-to-all | bytes 524288 | tf_op jit(solution)/shard_map/all_to_all | solution.py:13
  241.7 1.3 reduce.13
  243.4 1.4 convolution_bitcast_fusion.1
  245.2 5.8 %cholesky.16 = f32[64,64]{1,0:T(8,128)S(1)} custom-call(f32[64,64]{1,0:T(8,128)S(1)} %fusion.25), custom_call_target="Cholesky" | custom-call | tf_op jit(solution)/shard_map/jit(cholesky)/cholesky | solution.py:93
  251.1 0.6 compare_reduce_fusion
  251.7 0.7 fusion.21
  252.4 4.9 %custom-call.7 = f32[1,64,64]{1,2,0:T(8,128)S(1)} custom-call(f32[1,64,64]{2,1,0:T(8,128)S(1)} %fusion.21), custom_call_target="InvertDiagBlocksLowerTriangular" | custom-call | tf_op jit(solution)/shard_map/jit(_solve_triangular)/triangular_solve | solution.py:94
  257.6 0.7 fusion.23
  258.4 1.0 convolution_bitcast_fusion.2
  (44 shorter events, 5.1 us)
Async XLA Ops:
  0.6 187.5 %copy-start = (f32[1024,64]{0,1:T(8,128)S(1)}, f32[1024,64]{0,1:T(8,128)}, u32[]{:S(2)}) copy-start(f32[1024,64]{0,1:T(8,128)} %param.9) | copy-start | bytes 786436
  2.1 15.6 %all-to-all-start.1 = ((f32[8,1,256]{2,1,0:T(1,128)}), f32[8,1,256]{2,1,0:T(1,128)S(1)}, u32[]{:S(2)}, u32[]{:S(2)}) async-start(f32[8,1,256]{2,1,0:T(1,128)} %reshape.48), calls=%async_computation.1 | async-start | bytes 16384 | tf_op jit(solution)/shard_map/all_to_all | solution.py:13
  6.4 5.4 %copy-start.3 = (f32[32,16]{0,1:T(8,128)S(1)}, f32[32,16]{0,1:T(8,128)}, u32[]{:S(2)}) copy-start(f32[32,16]{0,1:T(8,128)} %param.8) | copy-start | bytes 6148
  16.3 1.4 copy-start.1
  17.7 32.0 %all-to-all-start = ((f32[8,128,8,4,16]{1,4,3,2,0:T(8,128)}), f32[8,128,8,4,16]{1,4,3,2,0:T(8,128)S(1)}, u32[]{:S(2)}, u32[]{:S(2)}) async-start(f32[8,128,8,4,16]{1,4,3,2,0:T(8,128)} %copy-done.1), calls=%async_computation | async-start | bytes 4194304 | tf_op jit(solution)/shard_map/all_to_all | solution.py:79
  52.1 5.2 %copy-start.4 = (f32[4,32]{1,0:T(4,128)S(1)}, f32[4,32]{1,0:T(4,128)}, u32[]{:S(2)}) copy-start(f32[4,32]{1,0:T(4,128)} %param.7) | copy-start | bytes 1540
  53.7 19.4 %all-to-all-start.2 = ((f32[128,32,4,16]{0,3,2,1:T(8,128)}), f32[128,32,4,16]{0,3,2,1:T(8,128)S(1)}, u32[]{:S(2)}, u32[]{:S(2)}) async-start(f32[128,32,4,16]{0,3,2,1:T(8,128)} %copy.57), calls=%async_computation.2 | async-start | bytes 2097152 | tf_op jit(solution)/shard_map/all_to_all | solution.py:82
  73.2 26.4 %all-to-all-start.4 = ((f32[32,1,128]{2,1,0:T(1,128)}), f32[32,1,128]{2,1,0:T(1,128)S(1)}, u32[]{:S(2)}, u32[]{:S(2)}) async-start(f32[32,1,128]{2,1,0:T(1,128)} %reshape.52), calls=%async_computation.4 | async-start | bytes 32768 | tf_op jit(solution)/shard_map/all_to_all | solution.py:13
  99.6 37.5 %all-to-all-start.3 = ((f32[32,1,8192]{2,1,0:T(1,128)}), f32[32,1,8192]{2,1,0:T(1,128)S(1)}, u32[]{:S(2)}, u32[]{:S(2)}) async-start(f32[32,1,8192]{2,1,0:T(1,128)} %reshape.50), calls=%async_computation.3 | async-start | bytes 2097152 | tf_op jit(solution)/shard_map/all_to_all | solution.py:84
  258.4 1.0 copy-start.2
